TPU v7x, 32 devices: a whole 2x2x4 slice. The times are simulated.
32 devices in a mesh: dp: 4 (over x, core), tensor: 8 (over z, y).
Axes of the slice: x: 2, y: 2, z: 4, core: 2. Of those that a mesh axis runs over, the one named last changes fastest.
Arguments:
- attn_ctx: bfloat16 [2048, 8192], P('dp', 'tensor'), may hold values from -6 to 6
- w_out: bfloat16 [8192, 8192], P('tensor'), may hold values from -0.09375 to 0.09375
- resid: bfloat16 [2048, 8192], P(('dp', 'tensor')), may hold values from -6 to 6
- teacher_gain: bfloat16 [8192], replicated, may hold values from 0.25 to 1.75
- dest_row: int32 [2048], replicated, may hold values from 0 to 2047, as said below
- student_in: bfloat16 [2048, 4096], P('dp', 'tensor'), may hold values from -6 to 6
- student_gain: bfloat16 [4096], replicated, may hold values from 0.25 to 1.75
- w_gate: bfloat16 [4096, 14336], P('dp', 'tensor'), may hold values from -0.09375 to 0.09375
- w_up: bfloat16 [4096, 14336], P('dp', 'tensor'), may hold values from -0.09375 to 0.09375
- w_down: bfloat16 [14336, 4096], P('tensor', 'dp'), may hold values from -0.0625 to 0.0625
- proj: bfloat16 [4096, 8192], P('dp', 'tensor'), may hold values from -0.09375 to 0.09375
Outputs:
- student_out: bfloat16 [2048, 4096], P('dp', 'tensor')
- row_loss: float32 [2048], P('dp')
- residue: float32 [2048, 8192], P('dp', 'tensor')
Inputs may be any that keep to these rules, and one draw needn't show every extreme that they name: A permutation of the rows; of the 64 rows i in one aligned block of teacher rows, at most 32 have dest_row[i] in any one tile of 512 student rows, and some tile receives exactly 32 of them.
All inputs are finite; a program needn't handle non-finite values.
Results may differ from a plain program's by a relative error of at most 0.012.
Values may be sent and summed in bfloat16 or wider, within the bound.
A program may use at most 192 MiB of HBM per device.

v0:
```python
import jax
import jax.numpy as jnp
from jax import lax
from jax.sharding import PartitionSpec as P

HT = 8192


def local(
    attn_ctx,
    w_out,
    resid,
    teacher_gain,
    dest_row,
    student_in,
    student_gain,
    w_gate,
    w_up,
    w_down,
    proj,
):
    tensor_count = lax.axis_size("tensor")
    group_count = lax.axis_size("dp")
    tile_rows = attn_ctx.shape[0]
    own_rows = resid.shape[0]
    portion = attn_ctx
    summed = lax.psum_scatter(
        jnp.dot(portion, w_out, preferred_element_type=jnp.float32).astype(jnp.bfloat16),
        "tensor",
        scatter_dimension=0,
        tiled=True,
    ).astype(jnp.float32)
    teacher_hidden = resid.astype(jnp.float32) + summed
    square_mean = jnp.mean(teacher_hidden * teacher_hidden, axis=1, keepdims=True)
    teacher_final = (
        teacher_hidden * lax.rsqrt(square_mean + 1e-06) * teacher_gain.astype(jnp.float32)
    ).astype(jnp.bfloat16)
    capacity = 2 * own_rows // group_count
    source_count = group_count * tensor_count
    group_ids = (dest_row // tile_rows).reshape(source_count, own_rows)
    onehot = (group_ids[:, :, None] == jnp.arange(group_count)[None, None, :]).astype(jnp.int32)
    slot_index = jnp.sum((jnp.cumsum(onehot, 1) - onehot) * onehot, 2)
    my_source = lax.axis_index("dp") * tensor_count + lax.axis_index("tensor")
    own_groups = lax.dynamic_index_in_dim(group_ids, my_source, 0, keepdims=False)
    own_slots = lax.dynamic_index_in_dim(slot_index, my_source, 0, keepdims=False)
    target_slot = own_groups * capacity + own_slots
    selector = (target_slot[None, :] == jnp.arange(group_count * capacity)[:, None]).astype(
        jnp.bfloat16
    )
    packed = jnp.dot(selector, teacher_final, preferred_element_type=jnp.float32).astype(
        jnp.bfloat16
    )
    col_width = teacher_final.shape[1] // tensor_count
    send_blocks = packed.reshape(group_count, capacity, tensor_count, col_width).transpose(
        0, 2, 1, 3
    )
    arrived = lax.all_to_all(
        lax.all_to_all(send_blocks, "dp", split_axis=0, concat_axis=0, tiled=True),
        "tensor",
        split_axis=1,
        concat_axis=1,
        tiled=True,
    )
    flattened = arrived.reshape(source_count * capacity, col_width)
    arrival_index = (jnp.arange(source_count)[:, None] * capacity + slot_index).reshape(-1)
    inverse = jnp.zeros(dest_row.shape, jnp.int32).at[dest_row].set(arrival_index)
    own_arrivals = lax.dynamic_slice_in_dim(inverse, lax.axis_index("dp") * tile_rows, tile_rows, 0)
    target = jnp.take(flattened, own_arrivals, axis=0)
    gathered = lax.all_gather(student_in, "tensor", axis=1, tiled=True)
    x_full = gathered.astype(jnp.float32)
    student_mean = jnp.mean(x_full * x_full, axis=1, keepdims=True)
    normed = (x_full * lax.rsqrt(student_mean + 1e-05) * student_gain.astype(jnp.float32)).astype(
        jnp.bfloat16
    )

    def add_rows(portion):
        return jnp.dot(normed, portion, preferred_element_type=jnp.float32)

    gate_acts = add_rows(lax.all_gather(w_gate, "dp", axis=0, tiled=True))
    up_acts = add_rows(lax.all_gather(w_up, "dp", axis=0, tiled=True))
    hidden = (jax.nn.silu(gate_acts) * up_acts).astype(jnp.bfloat16)
    partial_sum = jnp.dot(
        hidden, lax.all_gather(w_down, "dp", axis=1, tiled=True), preferred_element_type=jnp.float32
    )
    local_cols = student_in.shape[1]
    mlp_sum = lax.psum(partial_sum.astype(jnp.bfloat16), "tensor").astype(jnp.float32)
    out_full = (x_full + mlp_sum).astype(jnp.bfloat16)
    out_local = lax.dynamic_slice_in_dim(
        out_full, lax.axis_index("tensor") * local_cols, local_cols, 1
    )
    pred = jnp.dot(
        out_full, lax.all_gather(proj, "dp", axis=0, tiled=True), preferred_element_type=jnp.float32
    )
    residue = pred - target.astype(jnp.float32)
    row_error = jnp.sum(residue * residue, axis=1)
    row_loss = lax.psum(row_error, "tensor") / HT
    return (out_local, row_loss, residue)


def solution(mesh):
    placed = (
        P("dp", "tensor"),
        P("tensor", None),
        P(("dp", "tensor"), None),
        P(),
        P(),
        P("dp", "tensor"),
        P(),
        P("dp", "tensor"),
        P("dp", "tensor"),
        P("tensor", "dp"),
        P("dp", "tensor"),
    )
    return jax.shard_map(
        local,
        mesh=mesh,
        in_specs=placed,
        out_specs=(P("dp", "tensor"), P("dp"), P("dp", "tensor")),
        check_vma=False,
    )
```

profile of v0, /device:TPU:0, one launch (start us, length us, event | category | flops | bytes accessed | tf_op | source)
XLA Modules:
  0.0 813.1 jit_solution(8429802727703756237)
XLA Ops:
  7.2 0.0 copy-start
  7.2 0.0 all-gather.6.cloned.1.call-start
  7.2 0.7 all-gather.6.cloned.1.call-update
  7.9 0.0 all-gather.8.cloned.1.call-start
  8.0 0.7 all-gather.8.cloned.1.call-update
  8.7 0.0 all-gather.12.cloned.1.call-start
  8.7 0.7 all-gather.12.cloned.1.call-update
  9.4 0.0 all-gather.10.cloned.1.call-start
  9.4 0.5 all-gather.10.cloned.1.call-update
  10.0 0.0 reduce-scatter.2.cloned.1.call-start
  10.0 0.0 copy-done
  10.0 16.8 %convolution_convert_fusion = bf16[512,8192]{1,0:T(8,128)(2,1)} fusion(bf16[512,1024]{1,0:T(8,128)(2,1)S(1)} %copy-done, bf16[1024,8192]{1,0:T(8,128)(2,1)} %param.12), kind=kOutput, calls=%fused_computation.5 | convolution fusion | flops 8594128896 | bytes 26214400 | tf_op jit(solution)/shard_map/dot_general | solution.py:28
  26.8 0.0 copy-start.6
  26.8 0.0 reduce-scatter.2.cloned.1.call-update
  26.8 0.2 all-reduce.2.cloned.1.call-start
  27.1 0.4 copy-done.6
  27.5 59.9 %all-gather.6.cloned.1.call-done = bf16[512,4096]{1,0:T(8,128)(2,1)} async-done(((bf16[512,512]{1,0:T(8,128)(2,1)}), bf16[512,4096]{1,0:T(8,128)(2,1)}) %all-gather.6.cloned.1.call-update) | async-done | bytes 4194320 | tf_op jit(solution)/shard_map/all_gather | solution.py:69
  87.4 3.1 fusion
  90.5 90.7 %all-gather.8.cloned.1.call-done = bf16[4096,1792]{1,0:T(8,128)(2,1)} async-done(((bf16[1024,1792]{1,0:T(8,128)(2,1)}), bf16[4096,1792]{1,0:T(8,128)(2,1)}) %all-gather.8.cloned.1.call-update) | async-done | bytes 14680080 | tf_op jit(solution)/shard_map/all_gather | solution.py:79
  181.2 14.7 %fusion.11 = f32[512,1792]{1,0:T(8,128)} fusion(bf16[4096,1792]{1,0:T(8,128)(2,1)} %all-gather.8.cloned.1.call-done, bf16[512,4096]{1,0:T(8,128)(2,1)} %all-gather.6.cloned.1.call-done, f32[4096]{0:T(1024)S(1)} %convert_element_type.47, f32[512]{0:T(512)S(1)} %add_rsqrt_fusion), kind=kOutput, calls=%fused_computation.23 | convolution fusion | flops 7524581376 | bytes 22562816 | tf_op jit(solution)/shard_map/dot_general | solution.py:77
  195.8 80.9 %all-gather.12.cloned.1.call-done = bf16[1792,4096]{1,0:T(8,128)(2,1)} async-done(((bf16[1792,1024]{1,0:T(8,128)(2,1)}), bf16[1792,4096]{1,0:T(8,128)(2,1)}) %all-gather.12.cloned.1.call-update) | async-done | bytes 14680080 | tf_op jit(solution)/shard_map/all_gather | solution.py:83
  276.8 95.4 %all-gather.10.cloned.1.call-done = bf16[4096,1792]{1,0:T(8,128)(2,1)} async-done(((bf16[1024,1792]{1,0:T(8,128)(2,1)}), bf16[4096,1792]{1,0:T(8,128)(2,1)}) %all-gather.10.cloned.1.call-update) | async-done | bytes 14680080 | tf_op jit(solution)/shard_map/all_gather | solution.py:80
  372.2 28.8 %convolution_convert_fusion.2 = bf16[512,4096]{1,0:T(8,128)(2,1)} fusion(bf16[1792,4096]{1,0:T(8,128)(2,1)} %all-gather.12.cloned.1.call-done, f32[512,1792]{1,0:T(8,128)} %fusion.11, bf16[4096,1792]{1,0:T(8,128)(2,1)} %all-gather.10.cloned.1.call-done, bf16[512,4096]{1,0:T(8,128)(2,1)} %all-gather.6.cloned.1.call-done, f32[4096]{0:T(1024)S(1)} %convert_element_type.47, ...), kind=kOutput, calls=%fused_computation.11 | convolution fusion | flops 15048376320 | bytes 41437184 | tf_op jit(solution)/shard_map/dot_general | solution.py:82
  401.0 0.0 copy-start.5
  401.0 0.0 copy-start.7
  401.0 0.0 copy-start.3
  401.0 0.0 all-reduce.2.cloned.1.call-update
  401.0 0.3 all-gather.14.cloned.1.call-start
  401.3 0.5 all-gather.14.cloned.1.call-update
  401.8 0.0 copy-done.5
  401.8 0.0 copy-done.7
  401.8 0.1 eq.30
  401.9 0.1 copy.29
  402.0 1.7 select_reduce_fusion
  403.7 0.2 add_reduce_fusion
  403.9 119.3 %reduce-scatter.2.cloned.1.call-done = bf16[64,8192]{1,0:T(8,128)(2,1)} async-done(((bf16[512,8192]{1,0:T(8,128)(2,1)}), bf16[64,8192]{1,0:T(8,128)(2,1)}) %reduce-scatter.2.cloned.1.call-update) | async-done | bytes 1048592 | tf_op jit(solution)/shard_map/reduce_scatter | solution.py:27
  523.2 0.0 copy-done.3
  523.2 1.7 multiply_reduce_fusion.1
  524.9 2.0 convolution_convert_fusion.1
  526.9 1.4 copy.35
  528.3 1.2 copy.37
  529.5 28.2 %all_to_all.10 = bf16[4,8,32,1024]{3,2,1,0:T(8,128)(2,1)S(1)} all-to-all(bf16[4,8,32,1024]{3,2,1,0:T(8,128)(2,1)S(1)} %bitcast.17), channel_id=1, replica_groups=mesh['dp'=4,'tensor'=8] {'dp'}, dimensions={0} | all-to-all | bytes 4194304 | tf_op jit(solution)/shard_map/all_to_all | solution.py:58
  557.7 1.5 copy.33
  559.1 4.3 all-to-all-start.1
  563.5 0.1 copy.30
  563.6 0.1 broadcast_add_fusion
  563.6 0.1 reshape.60
  563.7 8.3 %scatter_custom_fusion = s32[2048]{0:T(1024)S(1)} fusion(s32[2048]{0:T(1024)S(1)} %get-tuple-element.5, s32[2048]{0:T(1024)S(1)} %reshape.60, s32[]{:T(128)} %constant.62.clone.1), kind=kCustom, calls=%fused_computation.43 | custom fusion | bytes 8196 | tf_op jit(solution)/shard_map/scatter | solution.py:66
  572.0 0.1 compare_and_fusion
  572.1 64.3 %all-to-all-done.1 = bf16[4,8,32,1024]{3,2,0,1:T(8,128)(2,1)} async-done(((bf16[4,8,32,1024]{3,2,0,1:T(8,128)(2,1)}), bf16[4,8,32,1024]{3,2,0,1:T(8,128)(2,1)}, u32[]{:S(2)}, u32[]{:S(2)}) %all-to-all-start.1) | async-done | bytes 2097184 | tf_op jit(solution)/shard_map/all_to_all | solution.py:57
  636.5 1.8 copy.34
  638.3 2.8 gather_fusion
  641.1 0.0 copy-start.4
  641.1 73.8 %all-reduce.2.cloned.1.call-done = bf16[512,4096]{1,0:T(8,128)(2,1)} async-done(((bf16[512,4096]{1,0:T(8,128)(2,1)}), bf16[512,4096]{1,0:T(8,128)(2,1)}) %all-reduce.2.cloned.1.call-update) | async-done | bytes 4194320 | tf_op jit(solution)/shard_map/psum | solution.py:86
  714.9 5.0 fusion.3
  719.9 0.0 copy-start.2
  719.9 1.9 copy-done.2
  721.8 0.8 constant_dynamic-slice_fusion
  722.7 51.0 %all-gather.14.cloned.1.call-done = bf16[4096,1024]{1,0:T(8,128)(2,1)} async-done(((bf16[1024,1024]{1,0:T(8,128)(2,1)}), bf16[4096,1024]{1,0:T(8,128)(2,1)}) %all-gather.14.cloned.1.call-update) | async-done | bytes 8388624 | tf_op jit(solution)/shard_map/all_gather | solution.py:92
  773.7 0.0 copy-done.4
  773.7 10.6 %multiply_reduce_fusion = (f32[512]{0:T(512)S(1)}, f32[512,1024]{1,0:T(8,128)}) fusion(bf16[512,1024]{1,0:T(8,128)(2,1)S(1)} %copy-done.4, pred[512]{0:T(512)(128)(4,1)S(1)} %get-tuple-element.3, bf16[512,4096]{1,0:T(8,128)(2,1)} %copy-done.2, bf16[4096,1024]{1,0:T(8,128)(2,1)} %all-gather.14.cloned.1.call-done), kind=kOutput, calls=%fused_computation.14 | convolution fusion | flops 4297588224 | bytes 15731200 | tf_op jit(solution)/shard_map/dot_general | solution.py:91
  784.3 21.3 %psum.15 = f32[512]{0:T(512)S(1)} all-reduce(f32[512]{0:T(512)S(1)} %get-tuple-element.7), channel_id=1, replica_groups=mesh['dp'=4,'tensor'=8] {'tensor'}, use_global_device_ids=true, to_apply=%region_8.9 | all-reduce | flops 512 | bytes 4096 | tf_op jit(solution)/shard_map/psum | solution.py:96
  805.6 0.6 broadcast_multiply_fusion
  806.2 0.0 copy-done.1
  (8 shorter events, 0.0 us)
Async XLA Ops:
  7.2 2.9 copy-start
  7.2 80.2 %all-gather.6.cloned.1.call-start = ((), (), s32[]{:S(2)}) async-start(), calls=%async_computation.3 | async-start | bytes 4718592 | tf_op jit(solution)/shard_map/all_gather | solution.py:69
  7.9 173.3 %all-gather.8.cloned.1.call-start = ((), (), s32[]{:S(2)}) async-start(), calls=%async_computation.4 | async-start | bytes 18350080 | tf_op jit(solution)/shard_map/all_gather | solution.py:79
  8.7 268.1 %all-gather.12.cloned.1.call-start = ((), (), s32[]{:S(2)}) async-start(), calls=%async_computation.6 | async-start | bytes 18350080 | tf_op jit(solution)/shard_map/all_gather | solution.py:83
  9.4 362.8 %all-gather.10.cloned.1.call-start = ((), (), s32[]{:S(2)}) async-start(), calls=%async_computation.5 | async-start | bytes 18350080 | tf_op jit(solution)/shard_map/all_gather | solution.py:80
  10.0 513.2 %reduce-scatter.2.cloned.1.call-start = ((), (), s32[]{:S(2)}) async-start(), calls=%async_computation.9 | async-start | bytes 9437184 | tf_op jit(solution)/shard_map/reduce_scatter | solution.py:27
  26.8 0.7 copy-start.6
  26.8 688.0 %all-reduce.2.cloned.1.call-start = ((), (), s32[]{:S(2)}) async-start(), calls=%async_computation.7 | async-start | bytes 8388608 | tf_op jit(solution)/shard_map/psum | solution.py:86
  401.0 0.8 copy-start.5
  401.0 0.8 copy-start.7
  401.0 122.2 %copy-start.3 = (bf16[64,8192]{1,0:T(8,128)(2,1)S(1)}, bf16[64,8192]{1,0:T(8,128)(2,1)}, u32[]{:S(2)}) copy-start(bf16[64,8192]{1,0:T(8,128)(2,1)} %param.13) | copy-start | bytes 3145732
  401.0 372.7 %all-gather.14.cloned.1.call-start = ((), (), s32[]{:S(2)}) async-start(), calls=%async_computation.8 | async-start | bytes 10485760 | tf_op jit(solution)/shard_map/all_gather | solution.py:92
  559.1 77.3 %all-to-all-start.1 = ((bf16[4,8,32,1024]{3,2,0,1:T(8,128)(2,1)}), bf16[4,8,32,1024]{3,2,0,1:T(8,128)(2,1)}, u32[]{:S(2)}, u32[]{:S(2)}) async-start(bf16[4,8,32,1024]{3,2,0,1:T(8,128)(2,1)} %copy.33), calls=%async_computation.2 | async-start | bytes 4194304 | tf_op jit(solution)/shard_map/all_to_all | solution.py:57
  641.1 132.7 %copy-start.4 = (bf16[512,1024]{1,0:T(8,128)(2,1)S(1)}, bf16[512,1024]{1,0:T(8,128)(2,1)}, u32[]{:S(2)}) copy-start(bf16[512,1024]{1,0:T(8,128)(2,1)} %gather_fusion) | copy-start | bytes 3145732
  719.9 2.0 copy-start.2
  773.7 32.5 %copy-start.1 = (bf16[512,1024]{1,0:T(8,128)(2,1)S(1)}, bf16[512,1024]{1,0:T(8,128)(2,1)}, u32[]{:S(2)}) copy-start(bf16[512,1024]{1,0:T(8,128)(2,1)} %param.11) | copy-start | bytes 3145732
Sparse Core Ops, SparseCore 0:
  10.0 77.3 all-gather.5
  89.0 92.1 all-gather.7
  182.8 93.9 all-gather.11
  278.2 93.9 all-gather.9
  375.7 147.4 reduce-scatter.1
  526.7 188.0 all-reduce.1
  716.4 57.2 all-gather.13
where the time goes:
time: 814 us; the launch traced here: 813 us
  waiting for transfers between devices  639 us (79%)
  matrix products  72.8 us (9%)
  blocking collectives  49.5 us (6%)
  local copies, waits for them, and re-layouts  20.5 us (3%)
  between operations  14.3 us (2%)
  other arithmetic  12.4 us (2%)
    reduce_scatter x1, waiting for transfers between devices, local(): lax.psum_scatter(jnp.dot(portion, w_out, preferred_element_type=jnp.float...  119 us
    all_gather x1, waiting for transfers between devices, local(): up_acts = add_rows(lax.all_gather(w_up, 'dp', axis=0, tiled=True))  95.4 us
    all_gather x1, waiting for transfers between devices, local(): gate_acts = add_rows(lax.all_gather(w_gate, 'dp', axis=0, tiled=True))  90.7 us
    all_gather x1, waiting for transfers between devices, local(): lax.all_gather(w_down, 'dp', axis=1, tiled=True)  80.9 us
    psum x1, waiting for transfers between devices, local(): lax.psum(partial_sum.astype(jnp.bfloat16), 'tensor').astype(jnp.float32)  73.8 us
    all_to_all x1, waiting for transfers between devices, local(): lax.all_to_all(lax.all_to_all(send_blocks, 'dp', split_axis=0, concat_axi...  64.3 us
    all_gather x1, waiting for transfers between devices, local(): gathered = lax.all_gather(student_in, 'tensor', axis=1, tiled=True)  59.9 us
    all_gather x1, waiting for transfers between devices, local(): lax.all_gather(proj, 'dp', axis=0, tiled=True)  51 us
  transfers between devices with their start and end apart: 8, of which 8 were waited for; matrix products, arithmetic and copies ran while one was open for 11% of the time, Pallas kernels for 0%

commit v1 on v0

--- a/solution.py
+++ b/solution.py
@@ -54,12 +54,20 @@
     send_blocks = packed.reshape(group_count, capacity, tensor_count, col_width).transpose(
         0, 2, 1, 3
     )
-    arrived = lax.all_to_all(
-        lax.all_to_all(send_blocks, "dp", split_axis=0, concat_axis=0, tiled=True),
-        "tensor",
-        split_axis=1,
-        concat_axis=1,
-        tiled=True,
+    arrived = jnp.concatenate(
+        lax.all_to_all(
+            jnp.stack(
+                jnp.split(
+                    lax.all_to_all(send_blocks, "dp", split_axis=0, concat_axis=0, tiled=True),
+                    lax.axis_size("tensor"),
+                    axis=1,
+                )
+            ),
+            "tensor",
+            0,
+            0,
+        ),
+        axis=1,
     )
     flattened = arrived.reshape(source_count * capacity, col_width)
     arrival_index = (jnp.arange(source_count)[:, None] * capacity + slot_index).reshape(-1)

time: 814 us -> 812 us (level)
  transfers between devices with their start and end apart: 8 -> 8, of which waited for: 8 -> 8; matrix products, arithmetic and copies ran while one was open for 11% -> 12% of each run, Pallas kernels for 0% -> 0%
where the time goes in v1:
time: 812 us
  waiting for transfers between devices  632 us (78%)
  matrix products  72.9 us (9%)
  blocking collectives  49.5 us (6%)
  local copies, waits for them, and re-layouts  26.1 us (3%)
  between operations  14.3 us (2%)
  other arithmetic  12.4 us (2%)
    reduce_scatter x1, waiting for transfers between devices, local(): lax.psum_scatter(jnp.dot(portion, w_out, preferred_element_type=jnp.float...  119 us
    all_gather x1, waiting for transfers between devices, local(): up_acts = add_rows(lax.all_gather(w_up, 'dp', axis=0, tiled=True))  95.4 us
    all_gather x1, waiting for transfers between devices, local(): gate_acts = add_rows(lax.all_gather(w_gate, 'dp', axis=0, tiled=True))  90.7 us
    all_gather x1, waiting for transfers between devices, local(): lax.all_gather(w_down, 'dp', axis=1, tiled=True)  80.8 us
    psum x1, waiting for transfers between devices, local(): lax.psum(partial_sum.astype(jnp.bfloat16), 'tensor').astype(jnp.float32)  71.1 us
    all_to_all x1, waiting for transfers between devices, local(): lax.all_to_all(jnp.stack(jnp.split(lax.all_to_all(send_blocks, 'dp', spli...  60.6 us
    all_gather x1, waiting for transfers between devices, local(): gathered = lax.all_gather(student_in, 'tensor', axis=1, tiled=True)  59.9 us
    all_gather x1, waiting for transfers between devices, local(): lax.all_gather(proj, 'dp', axis=0, tiled=True)  51 us
  transfers between devices with their start and end apart: 8, of which 8 were waited for; matrix products, arithmetic and copies ran while one was open for 12% of the time, Pallas kernels for 0%

profile of v1, /device:TPU:0, one launch (start us, length us, event | category | flops | bytes accessed | tf_op | source)
XLA Modules:
  0.0 811.6 jit_solution(995015661077062070)
XLA Ops:
  7.2 0.0 copy-start
  7.2 0.0 all-gather.6.cloned.1.call-start
  7.2 0.7 all-gather.6.cloned.1.call-update
  7.9 0.0 all-gather.8.cloned.1.call-start
  8.0 0.7 all-gather.8.cloned.1.call-update
  8.7 0.0 all-gather.12.cloned.1.call-start
  8.7 0.7 all-gather.12.cloned.1.call-update
  9.4 0.0 all-gather.10.cloned.1.call-start
  9.4 0.5 all-gather.10.cloned.1.call-update
  10.0 0.0 reduce-scatter.2.cloned.1.call-start
  10.0 0.0 copy-done
  10.0 16.8 %convolution_convert_fusion = bf16[512,8192]{1,0:T(8,128)(2,1)} fusion(bf16[512,1024]{1,0:T(8,128)(2,1)S(1)} %copy-done, bf16[1024,8192]{1,0:T(8,128)(2,1)} %param.12), kind=kOutput, calls=%fused_computation.5 | convolution fusion | flops 8594128896 | bytes 26214400 | tf_op jit(solution)/shard_map/dot_general | solution.py:28
  26.8 0.0 reduce-scatter.2.cloned.1.call-update
  26.9 0.2 all-reduce.2.cloned.1.call-start
  27.1 0.4 copy-done.7
  27.5 59.9 %all-gather.6.cloned.1.call-done = bf16[512,4096]{1,0:T(8,128)(2,1)} async-done(((bf16[512,512]{1,0:T(8,128)(2,1)}), bf16[512,4096]{1,0:T(8,128)(2,1)}) %all-gather.6.cloned.1.call-update) | async-done | bytes 4194320 | tf_op jit(solution)/shard_map/all_gather | solution.py:77
  87.4 3.1 fusion
  90.5 90.7 %all-gather.8.cloned.1.call-done = bf16[4096,1792]{1,0:T(8,128)(2,1)} async-done(((bf16[1024,1792]{1,0:T(8,128)(2,1)}), bf16[4096,1792]{1,0:T(8,128)(2,1)}) %all-gather.8.cloned.1.call-update) | async-done | bytes 14680080 | tf_op jit(solution)/shard_map/all_gather | solution.py:87
  181.2 14.8 %fusion.11 = f32[512,1792]{1,0:T(8,128)} fusion(bf16[4096,1792]{1,0:T(8,128)(2,1)} %all-gather.8.cloned.1.call-done, bf16[512,4096]{1,0:T(8,128)(2,1)} %all-gather.6.cloned.1.call-done, f32[4096]{0:T(1024)S(1)} %convert_element_type.47, f32[512]{0:T(512)S(1)} %add_rsqrt_fusion), kind=kOutput, calls=%fused_computation.23 | convolution fusion | flops 7524581376 | bytes 22562816 | tf_op jit(solution)/shard_map/dot_general | solution.py:85
  195.9 80.8 %all-gather.12.cloned.1.call-done = bf16[1792,4096]{1,0:T(8,128)(2,1)} async-done(((bf16[1792,1024]{1,0:T(8,128)(2,1)}), bf16[1792,4096]{1,0:T(8,128)(2,1)}) %all-gather.12.cloned.1.call-update) | async-done | bytes 14680080 | tf_op jit(solution)/shard_map/all_gather | solution.py:91
  276.8 95.4 %all-gather.10.cloned.1.call-done = bf16[4096,1792]{1,0:T(8,128)(2,1)} async-done(((bf16[1024,1792]{1,0:T(8,128)(2,1)}), bf16[4096,1792]{1,0:T(8,128)(2,1)}) %all-gather.10.cloned.1.call-update) | async-done | bytes 14680080 | tf_op jit(solution)/shard_map/all_gather | solution.py:88
  372.2 28.8 %convolution_convert_fusion.2 = bf16[512,4096]{1,0:T(8,128)(2,1)} fusion(bf16[1792,4096]{1,0:T(8,128)(2,1)} %all-gather.12.cloned.1.call-done, f32[512,1792]{1,0:T(8,128)} %fusion.11, bf16[4096,1792]{1,0:T(8,128)(2,1)} %all-gather.10.cloned.1.call-done, bf16[512,4096]{1,0:T(8,128)(2,1)} %all-gather.6.cloned.1.call-done, f32[4096]{0:T(1024)S(1)} %convert_element_type.47, ...), kind=kOutput, calls=%fused_computation.11 | convolution fusion | flops 15048376320 | bytes 41437184 | tf_op jit(solution)/shard_map/dot_general | solution.py:90
  401.0 0.0 all-reduce.2.cloned.1.call-update
  401.0 0.3 all-gather.14.cloned.1.call-start
  401.3 0.5 all-gather.14.cloned.1.call-update
  401.8 0.0 copy-done.6
  401.8 0.0 copy-done.8
  401.8 0.1 eq.30
  401.9 0.1 copy.49
  402.0 1.7 select_reduce_fusion
  403.7 0.2 add_reduce_fusion
  403.9 119.3 %reduce-scatter.2.cloned.1.call-done = bf16[64,8192]{1,0:T(8,128)(2,1)} async-done(((bf16[512,8192]{1,0:T(8,128)(2,1)}), bf16[64,8192]{1,0:T(8,128)(2,1)}) %reduce-scatter.2.cloned.1.call-update) | async-done | bytes 1048592 | tf_op jit(solution)/shard_map/reduce_scatter | solution.py:27
  523.2 1.7 multiply_reduce_fusion.1
  524.9 2.0 convolution_convert_fusion.1
  526.9 1.4 copy.70
  528.3 1.2 copy.72
  529.4 28.2 %all_to_all.10 = bf16[4,8,32,1024]{3,2,1,0:T(8,128)(2,1)S(1)} all-to-all(bf16[4,8,32,1024]{3,2,1,0:T(8,128)(2,1)S(1)} %bitcast.67), channel_id=1, replica_groups=mesh['dp'=4,'tensor'=8] {'dp'}, dimensions={0} | all-to-all | bytes 4194304 | tf_op jit(solution)/shard_map/all_to_all | solution.py:61
  557.6 0.7 fusion.23
  558.4 0.7 fusion.22
  559.1 0.7 fusion.21
  559.8 0.7 fusion.20
  560.5 0.7 fusion.19
  561.2 0.7 fusion.18
  562.0 0.7 fusion.17
  562.7 0.7 fusion.16
  563.4 3.7 all-to-all-start.1
  567.1 0.1 copy.50
  567.2 0.1 broadcast_add_fusion
  567.3 0.1 reshape.60
  567.3 8.3 %scatter_custom_fusion = s32[2048]{0:T(1024)S(1)} fusion(s32[2048]{0:T(1024)S(1)} %get-tuple-element.5, s32[2048]{0:T(1024)S(1)} %reshape.60, s32[]{:T(128)} %constant.62.clone.1), kind=kCustom, calls=%fused_computation.59 | custom fusion | bytes 8196 | tf_op jit(solution)/shard_map/scatter | solution.py:74
  575.7 0.1 compare_and_fusion
  575.8 60.6 %all-to-all-done.1 = bf16[8,4,1,32,1024]{4,3,1,2,0:T(8,128)(2,1)S(1)} async-done(((bf16[8,4,1,32,1024]{4,3,1,2,0:T(8,128)(2,1)}), bf16[8,4,1,32,1024]{4,3,1,2,0:T(8,128)(2,1)S(1)}, u32[]{:S(2)}, u32[]{:S(2)}) %all-to-all-start.1) | async-done | bytes 2097184 | tf_op jit(solution)/shard_map/all_to_all | solution.py:58
  636.4 1.3 copy-done.2
  637.7 1.8 copy.61
  639.5 2.8 gather_fusion
  642.3 71.1 %all-reduce.2.cloned.1.call-done = bf16[512,4096]{1,0:T(8,128)(2,1)} async-done(((bf16[512,4096]{1,0:T(8,128)(2,1)}), bf16[512,4096]{1,0:T(8,128)(2,1)}) %all-reduce.2.cloned.1.call-update) | async-done | bytes 4194320 | tf_op jit(solution)/shard_map/psum | solution.py:94
  713.4 5.0 fusion.3
  718.4 2.0 copy-done.3
  720.4 0.8 constant_dynamic-slice_fusion
  721.2 51.0 %all-gather.14.cloned.1.call-done = bf16[4096,1024]{1,0:T(8,128)(2,1)} async-done(((bf16[1024,1024]{1,0:T(8,128)(2,1)}), bf16[4096,1024]{1,0:T(8,128)(2,1)}) %all-gather.14.cloned.1.call-update) | async-done | bytes 8388624 | tf_op jit(solution)/shard_map/all_gather | solution.py:100
  772.2 0.0 copy-done.5
  772.2 10.6 %multiply_reduce_fusion = (f32[512]{0:T(512)S(1)}, f32[512,1024]{1,0:T(8,128)}) fusion(bf16[512,1024]{1,0:T(8,128)(2,1)S(1)} %copy-done.5, pred[512]{0:T(512)(128)(4,1)S(1)} %get-tuple-element.3, bf16[512,4096]{1,0:T(8,128)(2,1)} %copy-done.3, bf16[4096,1024]{1,0:T(8,128)(2,1)} %all-gather.14.cloned.1.call-done), kind=kOutput, calls=%fused_computation.14 | convolution fusion | flops 4297588224 | bytes 15731200 | tf_op jit(solution)/shard_map/dot_general | solution.py:99
  782.8 21.3 %psum.15 = f32[512]{0:T(512)S(1)} all-reduce(f32[512]{0:T(512)S(1)} %get-tuple-element.7), channel_id=1, replica_groups=mesh['dp'=4,'tensor'=8] {'tensor'}, use_global_device_ids=true, to_apply=%region_8.9 | all-reduce | flops 512 | bytes 4096 | tf_op jit(solution)/shard_map/psum | solution.py:104
  804.2 0.6 broadcast_multiply_fusion
  (17 shorter events, 0.1 us)
Async XLA Ops:
  7.2 2.9 copy-start
  7.2 80.2 %all-gather.6.cloned.1.call-start = ((), (), s32[]{:S(2)}) async-start(), calls=%async_computation.3 | async-start | bytes 4718592 | tf_op jit(solution)/shard_map/all_gather | solution.py:77
  7.9 173.3 %all-gather.8.cloned.1.call-start = ((), (), s32[]{:S(2)}) async-start(), calls=%async_computation.4 | async-start | bytes 18350080 | tf_op jit(solution)/shard_map/all_gather | solution.py:87
  8.7 268.1 %all-gather.12.cloned.1.call-start = ((), (), s32[]{:S(2)}) async-start(), calls=%async_computation.6 | async-start | bytes 18350080 | tf_op jit(solution)/shard_map/all_gather | solution.py:91
  9.4 362.8 %all-gather.10.cloned.1.call-start = ((), (), s32[]{:S(2)}) async-start(), calls=%async_computation.5 | async-start | bytes 18350080 | tf_op jit(solution)/shard_map/all_gather | solution.py:88
  10.0 513.2 %reduce-scatter.2.cloned.1.call-start = ((), (), s32[]{:S(2)}) async-start(), calls=%async_computation.9 | async-start | bytes 9437184 | tf_op jit(solution)/shard_map/reduce_scatter | solution.py:27
  26.8 0.7 copy-start.7
  26.9 686.5 %all-reduce.2.cloned.1.call-start = ((), (), s32[]{:S(2)}) async-start(), calls=%async_computation.7 | async-start | bytes 8388608 | tf_op jit(solution)/shard_map/psum | solution.py:94
  401.0 0.8 copy-start.6
  401.0 0.8 copy-start.8
  401.0 122.2 %copy-start.4 = (bf16[64,8192]{1,0:T(8,128)(2,1)S(1)}, bf16[64,8192]{1,0:T(8,128)(2,1)}, u32[]{:S(2)}) copy-start(bf16[64,8192]{1,0:T(8,128)(2,1)} %param.13) | copy-start | bytes 3145732
  401.0 371.2 %all-gather.14.cloned.1.call-start = ((), (), s32[]{:S(2)}) async-start(), calls=%async_computation.8 | async-start | bytes 10485760 | tf_op jit(solution)/shard_map/all_gather | solution.py:100
  563.4 73.0 %all-to-all-start.1 = ((bf16[8,4,1,32,1024]{4,3,1,2,0:T(8,128)(2,1)}), bf16[8,4,1,32,1024]{4,3,1,2,0:T(8,128)(2,1)S(1)}, u32[]{:S(2)}, u32[]{:S(2)}) async-start(bf16[8,4,1,32,1024]{4,3,1,2,0:T(8,128)(2,1)} %fusion.16), calls=%async_computation.2 | async-start | bytes 4194304 | tf_op jit(solution)/shard_map/all_to_all | solution.py:58
  636.4 1.3 copy-start.2
  642.3 129.9 %copy-start.5 = (bf16[512,1024]{1,0:T(8,128)(2,1)S(1)}, bf16[512,1024]{1,0:T(8,128)(2,1)}, u32[]{:S(2)}) copy-start(bf16[512,1024]{1,0:T(8,128)(2,1)} %gather_fusion) | copy-start | bytes 3145732
  718.4 2.0 copy-start.3
  772.2 32.5 %copy-start.1 = (bf16[512,1024]{1,0:T(8,128)(2,1)S(1)}, bf16[512,1024]{1,0:T(8,128)(2,1)}, u32[]{:S(2)}) copy-start(bf16[512,1024]{1,0:T(8,128)(2,1)} %param.11) | copy-start | bytes 3145732
Sparse Core Ops, SparseCore 0:
  10.0 77.3 all-gather.5
  89.0 92.1 all-gather.7
  182.7 93.9 all-gather.11
  278.2 93.9 all-gather.9
  375.7 147.4 reduce-scatter.1
  526.7 186.6 all-reduce.1
  714.9 57.2 all-gather.13
